TPU v7x, 512 devices: a whole 4x8x8 slice. The times are simulated.
512 devices in a mesh: gx: 32 (over y, x_hi, core), gy: 16 (over x_lo, z).
Axes of the slice: x: 4 (x_hi: 2, x_lo: 2; x = x_hi * 2 + x_lo), y: 8, z: 8, core: 2. Of those that a mesh axis runs over, the one named last changes fastest.
Arguments:
- prior_fields: bfloat16 [512, 64, 4096], P('gx', 'gy'), may hold values from -17 to 17
- measured_spread: bfloat16 [512, 16, 4096], P(None, 'gy', 'gx'), may hold values from -10 to 10
- scaled_misfit: bfloat16 [16, 4096], P('gy', 'gx'), may hold values from -12 to 12
- sensor_line_inside: int32 [16, 4096], P('gy', 'gx'), may hold values from 0 to 3
Outputs:
- analysis: bfloat16 [512, 64, 4096], P(None, 'gy', 'gx')
All inputs are finite; a program needn't handle non-finite values. Where the computation divides by a largest or mean magnitude, that divisor is 1e-20 or more.
Results may differ from a plain program's by a relative error of at most 0.0053.
Values may be sent and summed in bfloat16 or wider, within the bound.
A program may use at most 64 MiB of HBM per device.

v0:
```python
import jax
import jax.numpy as jnp
from jax import lax
from jax.sharding import Mesh
from jax.sharding import PartitionSpec as P

CP = 2
NEWTON = 2
GX = ("gx_0", "gx_1", "gx_2")


highest = lax.Precision.HIGHEST


def in_blocks(shard, dim, length):
    shape = shard.shape
    blocks = shard.reshape(*shape[:dim], length, shape[dim] // length, *shape[dim + 1 :])
    return jnp.moveaxis(blocks, dim, 0)


def joined_along(blocks, dim):
    blocks = jnp.moveaxis(blocks, 0, dim)
    shape = blocks.shape
    return blocks.reshape(*shape[:dim], shape[dim] * shape[dim + 1], *shape[dim + 2 :])


def turned_blocks(blocks, axes, order):
    inside = blocks.shape[1:]
    whole = blocks.reshape(*(lax.axis_size(a) for a in axes), *inside)
    for k in order:
        whole = lax.all_to_all(whole, axes[k], k, k, tiled=True)
    return whole.reshape(-1, *inside)


def two_step_exchange(shard, groups, order, split_dim, concat_dim):
    length = lax.axis_size(groups[0]) * lax.axis_size(groups[1])
    blocks = in_blocks(shard, split_dim, length)
    return joined_along(turned_blocks(blocks, groups, order), concat_dim)


def with_halo(shard, sides, width):
    for axis, dim in sides:
        size, length = (lax.axis_size(axis), shard.shape[dim])
        up = [(i, (i + 1) % size) for i in range(size - 1)]
        down = [(j, i) for i, j in up]
        last = lax.slice_in_dim(shard, length - width, length, axis=dim)
        leading = lax.slice_in_dim(shard, 0, width, axis=dim)
        before = lax.ppermute(last, axis, up)
        after = lax.ppermute(leading, axis, down)
        shard = jnp.concatenate([before, shard, after], axis=dim)
    return shard


def localize(positions, centre, radius):
    distance = (positions - centre) / radius
    return jnp.exp(-0.5 * distance * distance)


def newton_weights(gram_matrix, drive_vector, sweeps):
    sample_count = gram_matrix.shape[0]
    identity = jnp.eye(sample_count, dtype=jnp.float32)
    scaled_gram = identity + gram_matrix / (sample_count - 1.0)
    row_bound = jnp.max(jnp.sum(jnp.abs(scaled_gram), axis=1))
    iterate = scaled_gram / row_bound
    inverse = identity
    for newton_step in range(sweeps):
        if newton_step == 0:
            factor = 0.5 * (3.0 * identity - iterate)
            inverse = factor
        else:
            factor = 0.5 * (3.0 * identity - jnp.dot(inverse, iterate, precision=highest))
            inverse = jnp.dot(factor, inverse, precision=highest)
        if newton_step + 1 < sweeps:
            iterate = jnp.dot(iterate, factor, precision=highest)
    first_pass = jnp.dot(inverse, drive_vector, precision=highest)
    mean_weights = jnp.dot(inverse, first_pass, precision=highest) / (
        row_bound * (sample_count - 1.0)
    )
    return (inverse / jnp.sqrt(row_bound) + mean_weights[:, None]).astype(jnp.bfloat16)


def coarse_weights(obs_block, innov_block, positions, centre, radius):
    locality = localize(positions, centre, radius)
    scaled = (obs_block.astype(jnp.float32) * locality[None, :]).astype(jnp.bfloat16)
    gram_matrix = lax.dot_general(
        scaled, obs_block, (((1,), (1,)), ((), ())), preferred_element_type=jnp.float32
    )
    drive_vector = jnp.dot(scaled, innov_block, preferred_element_type=jnp.float32)
    return newton_weights(gram_matrix, drive_vector, NEWTON)


def hat_weights(row_centres, centre, spacing, height):
    clipped = jnp.clip(row_centres, 0.5 * spacing, height - 0.5 * spacing)
    return jnp.maximum(0.0, 1.0 - jnp.abs(clipped - centre) / spacing)


def apply_weights(transform, state_block, interp):
    sample_count, row_count, cell_count = state_block.shape
    product = lax.dot_general(
        transform,
        state_block.reshape(sample_count, row_count * cell_count),
        (((0,), (0,)), ((), ())),
        preferred_element_type=jnp.float32,
    )
    return product.reshape(sample_count, row_count, cell_count) * interp[None, :, None]


def on_device(prior_fields, measured_spread, scaled_misfit, sensor_line_inside):
    sorted_pieces = two_step_exchange(prior_fields, (("gx_0", "gx_1"), "gx_2"), (0, 1), 2, 0)
    sample_count, tile_rows, tile_cells = sorted_pieces.shape
    spacing = tile_rows // CP
    half_gap = spacing // 2
    height = tile_rows * lax.axis_size("gy")
    tile_index = lax.axis_index("gy")
    obs_rows = measured_spread.shape[1]
    packed = jnp.concatenate(
        [measured_spread, scaled_misfit[None], sensor_line_inside.astype(jnp.bfloat16)[None]],
        axis=0,
    )
    nearby = with_halo(packed, (("gy", 1),), obs_rows)
    obs_block = nearby[:sample_count].reshape(sample_count, -1)
    innov_block = nearby[sample_count].reshape(-1)
    tile_offset = jnp.arange(3 * obs_rows, dtype=jnp.int32) // obs_rows - 1
    base_rows = ((tile_index + tile_offset) * tile_rows).astype(jnp.float32)
    positions = (base_rows[:, None] + nearby[sample_count + 1].astype(jnp.float32) + 0.5).reshape(
        -1
    )
    own_list = []
    for point_slot in range(CP):
        centre = ((tile_index * CP + point_slot).astype(jnp.float32) + 0.5) * spacing
        own_list.append(coarse_weights(obs_block, innov_block, positions, centre, float(tile_rows)))
    own_weights = jnp.stack(own_list)
    state_mean = jnp.sum(sorted_pieces, axis=0, dtype=jnp.float32) / sample_count
    deviation = (sorted_pieces.astype(jnp.float32) - state_mean[None]).astype(jnp.bfloat16)

    def centres_of(first_row, last_row):
        return (tile_index * tile_rows + jnp.arange(first_row, last_row, dtype=jnp.int32)).astype(
            jnp.float32
        ) + 0.5

    def centre_of(column):
        return ((tile_index * CP + column - 1).astype(jnp.float32) + 0.5) * spacing

    increment = jnp.zeros((sample_count, tile_rows, tile_cells), jnp.float32)
    for column in range(1, CP + 1):
        first_row = max(0, (column - 1) * spacing - half_gap)
        last_row = min(tile_rows, (column - 1) * spacing + spacing + half_gap)
        interp = hat_weights(centres_of(first_row, last_row), centre_of(column), spacing, height)
        increment = increment.at[:, first_row:last_row].add(
            apply_weights(own_weights[column - 1], deviation[:, first_row:last_row], interp)
        )
    state_rims = with_halo(deviation, (("gy", 1),), half_gap)
    below_rows = state_rims[:, :half_gap]
    above_rows = state_rims[:, tile_rows + half_gap :]
    below_interp = hat_weights(centres_of(-half_gap, 0), centre_of(1), spacing, height)
    above_interp = hat_weights(
        centres_of(tile_rows, tile_rows + half_gap), centre_of(CP), spacing, height
    )
    for_previous = apply_weights(own_weights[0], below_rows, below_interp)
    for_next = apply_weights(own_weights[CP - 1], above_rows, above_interp)
    returned = with_halo(
        jnp.concatenate([for_previous, for_next], axis=1).astype(jnp.bfloat16),
        (("gy", 1),),
        half_gap,
    ).astype(jnp.float32)
    increment = increment.at[:, :half_gap].add(returned[:, :half_gap])
    increment = increment.at[:, tile_rows - half_gap :].add(returned[:, 3 * half_gap :])
    return (state_mean[None] + increment).astype(jnp.bfloat16)


def solution(mesh):
    finer = Mesh(mesh.devices.reshape(8, 2, 2, mesh.shape["gy"]), ("gx_0", "gx_1", "gx_2", "gy"))
    return jax.shard_map(
        on_device,
        mesh=finer,
        in_specs=(P(GX, "gy", None), P(None, "gy", GX), P("gy", GX), P("gy", GX)),
        out_specs=P(None, "gy", GX),
        check_vma=False,
    )
```

profile of v0, /device:TPU:6, one launch (start us, length us, event | category | flops | bytes accessed | tf_op | source)
XLA Modules:
  0.0 94.2 jit_solution(1974699716554060294)
XLA Ops:
  0.0 0.7 convert_bitcast_fusion
  0.7 0.0 copy-start.1
  0.7 0.7 copy-done.1
  1.3 0.9 pad_maximum_fusion.1
  2.2 4.3 %collective-permute-start = (bf16[514,1,128]{2,0,1:T(8,128)(2,1)S(1)}, bf16[514,1,128]{2,0,1:T(8,128)(2,1)S(1)}, u32[]{:S(2)}, u32[]{:S(2)}) collective-permute-start(bf16[514,1,128]{2,0,1:T(8,128)(2,1)S(1)} %pad_maximum_fusion.1), channel_id=1, source_target_pairs={{0,1},{1,2},{2,3},{3,4},{4,5},{5,6},{6,7},{7,8},{8,9},{9,10},{10,1... | collective-permute-start | bytes 394760 | tf_op jit(solution)/shard_map/ppermute | solution.py:48
  6.5 8.9 %collective-permute-start.1 = (bf16[514,1,128]{2,0,1:T(8,128)(2,1)S(1)}, bf16[514,1,128]{2,0,1:T(8,128)(2,1)S(1)}, u32[]{:S(2)}, u32[]{:S(2)}) collective-permute-start(bf16[514,1,128]{2,0,1:T(8,128)(2,1)S(1)} %pad_maximum_fusion.1), channel_id=1, source_target_pairs={{1,0},{2,1},{3,2},{4,3},{5,4},{6,5},{7,6},{8,7},{9,8},{10,9},{11,1... | collective-permute-start | bytes 394760 | tf_op jit(solution)/shard_map/ppermute | solution.py:49
  15.4 1.6 %reshape.304 = bf16[16,4,32,128]{3,2,1,0:T(8,128)(2,1)S(1)} reshape(bf16[16,4,4096]{2,1,0:T(4,128)(2,1)} %param.12) | data formatting | bytes 1048576 | tf_op jit(solution)/shard_map/reshape | solution.py:17
  17.0 1.4 %copy.50 = bf16[16,2,16,4,128]{4,2,1,3,0:T(8,128)(2,1)} copy(bf16[16,2,16,4,128]{4,1,0,3,2:T(2,128)(2,1)S(1)} %bitcast.103) | data formatting | bytes 1048576 | tf_op jit(solution)/shard_map/reshape | solution.py:29
  18.4 0.0 copy-start
  18.4 10.2 %all-to-all-start = ((bf16[16,2,16,4,128]{4,2,1,3,0:T(8,128)(2,1)}), bf16[16,2,16,4,128]{4,2,1,3,0:T(8,128)(2,1)}, u32[]{:S(2)}, u32[]{:S(2)}) async-start(bf16[16,2,16,4,128]{4,2,1,3,0:T(8,128)(2,1)} %copy.50), calls=%async_computation | async-start | bytes 1048576 | tf_op jit(solution)/shard_map/all_to_all | solution.py:31
  28.7 0.0 collective-permute-done
  28.7 0.0 collective-permute-done.1
  28.7 0.0 copy-done
  28.7 0.1 multiply_exponential_fusion
  28.8 0.1 fusion.24
  29.0 1.5 %abs_reduce_fusion = (f32[512]{0:T(512)S(1)}, f32[512,512]{0,1:T(8,128)}) fusion(bf16[512,3,128]{2,0,1:T(8,128)(2,1)S(1)} %get-tuple-element.57, bf16[514,3,128]{2,0,1:T(8,128)(2,1)S(1)} %pad_maximum_fusion), kind=kOutput, calls=%fused_computation.36 | convolution fusion | flops 202898944 | bytes 1837056 | tf_op jit(solution)/shard_map/dot_general | solution.py:85
  30.5 0.2 copy.60
  30.7 0.5 abs_reduce_fusion.1
  31.2 0.0 copy-start.2
  31.2 0.2 copy.55
  31.4 0.7 reduce_max.19
  32.1 0.0 copy-start.3
  32.1 5.9 %fusion.20 = f32[512,512]{1,0:T(8,128)S(1)} fusion(f32[512,512]{0,1:T(8,128)} %get-tuple-element.66, f32[]{:T(128)} %reduce_max.19), kind=kOutput, calls=%fused_computation.31 | convolution fusion | flops 1612185600 | bytes 2097156 | tf_op jit(solution)/shard_map/dot_general | solution.py:74
  38.0 0.0 copy-done.3
  38.1 2.7 %fusion.3 = f32[512,512]{0,1:T(8,128)S(1)} fusion(f32[512,512]{1,0:T(8,128)S(1)} %fusion.20, f32[512,512]{0,1:T(8,128)S(1)} %copy-done.3, f32[]{:T(128)} %reduce_max.19), kind=kOutput, calls=%fused_computation.11 | convolution fusion | flops 1612972032 | bytes 3145732 | tf_op jit(solution)/shard_map/dot_general | solution.py:71
  40.8 4.2 %fusion.17 = f32[512,512]{1,0:T(8,128)S(1)} fusion(f32[512,512]{0,1:T(8,128)S(1)} %fusion.3, f32[512,512]{0,1:T(8,128)S(1)} %copy-done.3, f32[]{:T(128)} %reduce_max.19), kind=kOutput, calls=%fused_computation.30 | convolution fusion | flops 1611923456 | bytes 3145732 | tf_op jit(solution)/shard_map/dot_general | solution.py:72
  45.0 0.2 convolution_bitcast_fusion.3
  45.2 1.0 %convolution_bitcast_fusion.2 = f32[512,1]{0,1:T(1,128)S(1)} fusion(f32[512,512]{1,0:T(8,128)S(1)} %fusion.17, f32[512,1]{0,1:T(1,128)S(1)} %convolution_bitcast_fusion.3), kind=kOutput, calls=%fused_computation.22 | convolution fusion | flops 3145728 | bytes 1052672 | tf_op jit(solution)/shard_map/dot_general | solution.py:75
  46.2 1.0 %fusion.75 = f32[1,512]{1,0:T(1,128)S(1)} fusion(f32[512,512]{1,0:T(8,128)S(1)} %fusion.17, f32[512,1]{0,1:T(1,128)S(1)} %convolution_bitcast_fusion.2), kind=kOutput, calls=%fused_computation.116 | convolution fusion | flops 3145728 | bytes 1052672 | tf_op jit(solution)/shard_map/dot_general | solution.py:76
  47.2 0.7 reduce_max.18
  47.9 4.4 %fusion.14 = f32[512,512]{1,0:T(8,128)S(1)} fusion(f32[512,512]{0,1:T(8,128)S(1)} %get-tuple-element.64, f32[]{:T(128)} %reduce_max.18), kind=kOutput, calls=%fused_computation.28 | convolution fusion | flops 1612185600 | bytes 2097156 | tf_op jit(solution)/shard_map/dot_general | solution.py:74
  52.2 0.0 copy-done.2
  52.2 2.7 %fusion.2 = f32[512,512]{0,1:T(8,128)S(1)} fusion(f32[512,512]{1,0:T(8,128)S(1)} %fusion.14, f32[512,512]{0,1:T(8,128)S(1)} %get-tuple-element.64, f32[]{:T(128)} %reduce_max.18), kind=kOutput, calls=%fused_computation.10 | convolution fusion | flops 1612972032 | bytes 3145732 | tf_op jit(solution)/shard_map/dot_general | solution.py:71
  55.0 5.5 %fusion.11 = f32[512,512]{1,0:T(8,128)S(1)} fusion(f32[512,512]{0,1:T(8,128)S(1)} %fusion.2, f32[512,512]{0,1:T(8,128)} %copy-done.2, f32[]{:T(128)} %reduce_max.18), kind=kOutput, calls=%fused_computation.27 | convolution fusion | flops 1611923456 | bytes 3145732 | tf_op jit(solution)/shard_map/dot_general | solution.py:72
  60.4 0.2 convolution_bitcast_fusion.5
  60.6 1.0 %convolution_bitcast_fusion.4 = f32[512,1]{0,1:T(1,128)S(1)} fusion(f32[512,512]{1,0:T(8,128)S(1)} %fusion.11, f32[512,1]{0,1:T(1,128)S(1)} %convolution_bitcast_fusion.5), kind=kOutput, calls=%fused_computation.24 | convolution fusion | flops 3145728 | bytes 1052672 | tf_op jit(solution)/shard_map/dot_general | solution.py:75
  61.6 1.0 %fusion.74 = f32[1,512]{1,0:T(1,128)S(1)} fusion(f32[512,512]{1,0:T(8,128)S(1)} %fusion.11, f32[512,1]{0,1:T(1,128)S(1)} %convolution_bitcast_fusion.4), kind=kOutput, calls=%fused_computation.115 | convolution fusion | flops 3145728 | bytes 1052672 | tf_op jit(solution)/shard_map/dot_general | solution.py:76
  65.5 0.2 add_convert_fusion.1
  65.6 0.2 add_convert_fusion.2
  65.8 0.0 all-to-all-done
  65.8 1.1 %copy.51 = bf16[16,2,16,4,128]{4,2,0,3,1:T(8,128)(2,1)S(1)} copy(bf16[16,2,16,4,128]{4,2,1,3,0:T(8,128)(2,1)} %all-to-all-done) | data formatting | bytes 1048576 | tf_op jit(solution)/shard_map/all_to_all | solution.py:31
  66.9 4.2 %all_to_all.10 = bf16[16,2,16,4,128]{4,2,0,3,1:T(8,128)(2,1)S(1)} all-to-all(bf16[16,2,16,4,128]{4,2,0,3,1:T(8,128)(2,1)S(1)} %copy.51), channel_id=1, replica_groups=mesh['gx_0'=8,'gx_1'=2,'gx_2'=2,'gy'=16] {'gx_2'}, dimensions={1} | all-to-all | bytes 1048576 | tf_op jit(solution)/shard_map/all_to_all | solution.py:31
  71.0 0.1 convert_reduce_fusion
  71.1 0.1 copy.56
  71.3 0.1 fusion.22
  71.4 0.1 fusion.73
  71.5 3.9 %collective-permute-start.2 = (bf16[512,1,128]{2,0,1:T(8,128)(2,1)S(1)}, bf16[512,1,128]{2,0,1:T(8,128)(2,1)}, u32[]{:S(2)}, u32[]{:S(2)}) collective-permute-start(bf16[512,1,128]{2,0,1:T(8,128)(2,1)S(1)} %get-tuple-element.53), channel_id=1, source_target_pairs={{1,0},{2,1},{3,2},{4,3},{5,4},{6,5},{7,6},{8,7},{9,8},{10,9},{11,1... | collective-permute-start | bytes 393224 | tf_op jit(solution)/shard_map/ppermute | solution.py:49
  75.4 0.2 copy.57
  75.6 0.5 convolution_multiply_fusion.1
  76.1 0.1 scatter-add.14
  76.2 0.2 copy.61
  76.4 1.9 %collective-permute-start.4 = (bf16[512,1,128]{2,0,1:T(8,128)(2,1)S(1)}, bf16[512,1,128]{2,0,1:T(8,128)(2,1)S(1)}, u32[]{:S(2)}, u32[]{:S(2)}) collective-permute-start(bf16[512,1,128]{2,0,1:T(8,128)(2,1)S(1)} %get-tuple-element.54), channel_id=1, source_target_pairs={{0,1},{1,2},{2,3},{3,4},{4,5},{5,6},{6,7},{7,8},{8,9},{9,10},{10,1... | collective-permute-start | bytes 393224 | tf_op jit(solution)/shard_map/ppermute | solution.py:48
  78.3 0.7 collective-permute-done.2
  79.0 1.3 %fusion.9 = bf16[512,1,128]{2,0,1:T(8,128)(2,1)S(1)} fusion(bf16[512,512]{1,0:T(8,128)(2,1)S(1)} %add_convert_fusion.1, bf16[512,1,128]{2,0,1:T(8,128)(2,1)} %collective-permute-done.2, f32[]{:T(128)S(6)} %max.50), kind=kOutput, calls=%fused_computation.21 | convolution fusion | flops 67239936 | bytes 786436 | tf_op jit(solution)/shard_map/dot_general | solution.py:99
  80.3 1.9 %collective-permute-start.3 = (bf16[512,1,128]{2,0,1:T(8,128)(2,1)S(1)}, bf16[512,1,128]{2,0,1:T(8,128)(2,1)S(1)}, u32[]{:S(2)}, u32[]{:S(2)}) collective-permute-start(bf16[512,1,128]{2,0,1:T(8,128)(2,1)S(1)} %fusion.9), channel_id=1, source_target_pairs={{0,1},{1,2},{2,3},{3,4},{4,5},{5,6},{6,7},{7,8},{8,9},{9,10},{10,1... | collective-permute-start | bytes 393224 | tf_op jit(solution)/shard_map/ppermute | solution.py:48
  82.2 3.4 %collective-permute-done.4 = bf16[512,1,128]{2,0,1:T(8,128)(2,1)S(1)} collective-permute-done((bf16[512,1,128]{2,0,1:T(8,128)(2,1)S(1)}, bf16[512,1,128]{2,0,1:T(8,128)(2,1)S(1)}, u32[]{:S(2)}, u32[]{:S(2)}) %collective-permute-start.4) | collective-permute-done | bytes 131104 | tf_op jit(solution)/shard_map/ppermute | solution.py:48
  85.6 0.3 fusion.8
  86.0 2.6 %collective-permute-start.5 = (bf16[512,1,128]{2,0,1:T(8,128)(2,1)S(1)}, bf16[512,1,128]{2,0,1:T(8,128)(2,1)S(1)}, u32[]{:S(2)}, u32[]{:S(2)}) collective-permute-start(bf16[512,1,128]{2,0,1:T(8,128)(2,1)S(1)} %fusion.8), channel_id=1, source_target_pairs={{1,0},{2,1},{3,2},{4,3},{5,4},{6,5},{7,6},{8,7},{9,8},{10,9},{11,1... | collective-permute-start | bytes 393224 | tf_op jit(solution)/shard_map/ppermute | solution.py:49
  88.6 0.5 fusion.5
  89.1 0.1 collective-permute-done.3
  89.2 3.6 %collective-permute-done.5 = bf16[512,1,128]{2,0,1:T(8,128)(2,1)S(1)} collective-permute-done((bf16[512,1,128]{2,0,1:T(8,128)(2,1)S(1)}, bf16[512,1,128]{2,0,1:T(8,128)(2,1)S(1)}, u32[]{:S(2)}, u32[]{:S(2)}) %collective-permute-start.5) | collective-permute-done | bytes 131104 | tf_op jit(solution)/shard_map/ppermute | solution.py:49
  92.9 0.1 add_convert_fusion
  93.0 1.2 %copy.63 = bf16[512,4,128]{2,1,0:T(4,128)(2,1)} copy(bf16[512,4,128]{2,0,1:T(8,128)(2,1)S(1)} %add_convert_fusion) | data formatting | bytes 1048576 | tf_op jit(solution)/shard_map/convert_element_type | solution.py:168
  (11 shorter events, 0.2 us)
Async XLA Ops:
  0.7 0.7 copy-start.1
  2.2 26.4 %collective-permute-start = (bf16[514,1,128]{2,0,1:T(8,128)(2,1)S(1)}, bf16[514,1,128]{2,0,1:T(8,128)(2,1)S(1)}, u32[]{:S(2)}, u32[]{:S(2)}) collective-permute-start(bf16[514,1,128]{2,0,1:T(8,128)(2,1)S(1)} %pad_maximum_fusion.1), channel_id=1, source_target_pairs={{0,1},{1,2},{2,3},{3,4},{4,5},{5,6},{6,7},{7,8},{8,9},{9,10},{10,1... | collective-permute-start | bytes 394760 | tf_op jit(solution)/shard_map/ppermute | solution.py:48
  6.5 22.2 %collective-permute-start.1 = (bf16[514,1,128]{2,0,1:T(8,128)(2,1)S(1)}, bf16[514,1,128]{2,0,1:T(8,128)(2,1)S(1)}, u32[]{:S(2)}, u32[]{:S(2)}) collective-permute-start(bf16[514,1,128]{2,0,1:T(8,128)(2,1)S(1)} %pad_maximum_fusion.1), channel_id=1, source_target_pairs={{1,0},{2,1},{3,2},{4,3},{5,4},{6,5},{7,6},{8,7},{9,8},{10,9},{11,1... | collective-permute-start | bytes 394760 | tf_op jit(solution)/shard_map/ppermute | solution.py:49
  18.4 10.3 %copy-start = (bf16[512,1,128]{2,0,1:T(8,128)(2,1)S(1)}, bf16[512,1,128]{2,0,1:T(8,128)(2,1)}, u32[]{:S(2)}) copy-start(bf16[512,1,128]{2,0,1:T(8,128)(2,1)} %param.13) | copy-start | bytes 393220
  18.4 47.4 %all-to-all-start = ((bf16[16,2,16,4,128]{4,2,1,3,0:T(8,128)(2,1)}), bf16[16,2,16,4,128]{4,2,1,3,0:T(8,128)(2,1)}, u32[]{:S(2)}, u32[]{:S(2)}) async-start(bf16[16,2,16,4,128]{4,2,1,3,0:T(8,128)(2,1)} %copy.50), calls=%async_computation | async-start | bytes 1048576 | tf_op jit(solution)/shard_map/all_to_all | solution.py:31
  31.2 21.1 %copy-start.2 = (f32[512,512]{0,1:T(8,128)}, f32[512,512]{0,1:T(8,128)S(1)}, u32[]{:S(2)}) copy-start(f32[512,512]{0,1:T(8,128)S(1)} %get-tuple-element.64) | copy-start | bytes 3145732
  32.1 5.9 %copy-start.3 = (f32[512,512]{0,1:T(8,128)S(1)}, f32[512,512]{0,1:T(8,128)}, u32[]{:S(2)}) copy-start(f32[512,512]{0,1:T(8,128)} %get-tuple-element.66) | copy-start | bytes 3145732
  71.5 7.5 %collective-permute-start.2 = (bf16[512,1,128]{2,0,1:T(8,128)(2,1)S(1)}, bf16[512,1,128]{2,0,1:T(8,128)(2,1)}, u32[]{:S(2)}, u32[]{:S(2)}) collective-permute-start(bf16[512,1,128]{2,0,1:T(8,128)(2,1)S(1)} %get-tuple-element.53), channel_id=1, source_target_pairs={{1,0},{2,1},{3,2},{4,3},{5,4},{6,5},{7,6},{8,7},{9,8},{10,9},{11,1... | collective-permute-start | bytes 393224 | tf_op jit(solution)/shard_map/ppermute | solution.py:49
  76.4 9.3 %collective-permute-start.4 = (bf16[512,1,128]{2,0,1:T(8,128)(2,1)S(1)}, bf16[512,1,128]{2,0,1:T(8,128)(2,1)S(1)}, u32[]{:S(2)}, u32[]{:S(2)}) collective-permute-start(bf16[512,1,128]{2,0,1:T(8,128)(2,1)S(1)} %get-tuple-element.54), channel_id=1, source_target_pairs={{0,1},{1,2},{2,3},{3,4},{4,5},{5,6},{6,7},{7,8},{8,9},{9,10},{10,1... | collective-permute-start | bytes 393224 | tf_op jit(solution)/shard_map/ppermute | solution.py:48
  80.3 9.0 %collective-permute-start.3 = (bf16[512,1,128]{2,0,1:T(8,128)(2,1)S(1)}, bf16[512,1,128]{2,0,1:T(8,128)(2,1)S(1)}, u32[]{:S(2)}, u32[]{:S(2)}) collective-permute-start(bf16[512,1,128]{2,0,1:T(8,128)(2,1)S(1)} %fusion.9), channel_id=1, source_target_pairs={{0,1},{1,2},{2,3},{3,4},{4,5},{5,6},{6,7},{7,8},{8,9},{9,10},{10,1... | collective-permute-start | bytes 393224 | tf_op jit(solution)/shard_map/ppermute | solution.py:48
  86.0 6.9 %collective-permute-start.5 = (bf16[512,1,128]{2,0,1:T(8,128)(2,1)S(1)}, bf16[512,1,128]{2,0,1:T(8,128)(2,1)S(1)}, u32[]{:S(2)}, u32[]{:S(2)}) collective-permute-start(bf16[512,1,128]{2,0,1:T(8,128)(2,1)S(1)} %fusion.8), channel_id=1, source_target_pairs={{1,0},{2,1},{3,2},{4,3},{5,4},{6,5},{7,6},{8,7},{9,8},{10,9},{11,1... | collective-permute-start | bytes 393224 | tf_op jit(solution)/shard_map/ppermute | solution.py:49
where the time goes:
time: 94.9 us; the launch traced here: 94.2 us
  matrix products  34.3 us (36%)
  starting transfers between devices  33.7 us (36%)
  waiting for transfers between devices  7.85 us (8%)
  local copies, waits for them, and re-layouts  6.97 us (7%)
  blocking collectives  4.15 us (4%)
  other arithmetic  3.98 us (4%)
  between operations  3.23 us (3%)
    ppermute x3, starting transfers between devices, with_halo(): after = lax.ppermute(leading, axis, down)  15.4 us
    dot_general x2, matrix products, newton_weights(): iterate = jnp.dot(iterate, factor, precision=highest)  10.3 us
    all_to_all x1, starting transfers between devices, turned_blocks(): whole = lax.all_to_all(whole, axes[k], k, k, tiled=True)  10.2 us
    dot_general x2, matrix products, newton_weights(): inverse = jnp.dot(factor, inverse, precision=highest)  9.71 us
    ppermute x3, starting transfers between devices, with_halo(): before = lax.ppermute(last, axis, up)  8.12 us
    dot_general x2, matrix products, newton_weights(): jnp.dot(inverse, iterate, precision=highest)  5.44 us
    ppermute x3, waiting for transfers between devices, with_halo(): after = lax.ppermute(leading, axis, down)  4.31 us
    all_to_all x1, blocking collectives, turned_blocks(): whole = lax.all_to_all(whole, axes[k], k, k, tiled=True)  4.15 us
  transfers between devices with their start and end apart: 7, of which 4 were waited for; matrix products, arithmetic and copies ran while one was open for 43% of the time, Pallas kernels for 0%

commit v1 on v0

v1 whole, which is shorter than its diff:
```python
import functools

import jax
import jax.numpy as jnp
from jax import lax
from jax.experimental import pallas as pl
from jax.experimental.pallas import tpu as pltpu
from jax.sharding import PartitionSpec as P

MESH = pl.DeviceIdType.MESH
NT = (((1,), (1,)), ((), ()))
NN = (((1,), (0,)), ((), ()))


def mm(a, b, dims=NN):
    return lax.dot_general(a, b, dims, preferred_element_type=jnp.float32)


def halves(x):
    high = x.astype(jnp.bfloat16)
    low = (x - high.astype(jnp.float32)).astype(jnp.bfloat16)
    return high, low


def hat(row, point, spacing, height):
    r = jnp.clip(row.astype(jnp.float32) + 0.5, 0.5 * spacing, height - 0.5 * spacing)
    centre = (point.astype(jnp.float32) + 0.5) * spacing
    return jnp.maximum(0.0, 1.0 - jnp.abs(r - centre) / spacing)


def kernel(
    n_gx,
    n_gy,
    prior_ref,
    spread_ref,
    misfit_ref,
    line_ref,
    out_ref,
    recv,
    obs,
    obs_misfit,
    obs_line,
    transforms,
    mixed,
    wide,
    a2a_send,
    a2a_recv,
    obs_send,
    obs_recv,
    own_sem,
):
    gx = lax.axis_index("gx")
    gy = lax.axis_index("gy")
    own_members, rows, _ = prior_ref.shape
    members, lanes = spread_ref.shape
    spacing = rows // 2
    height = rows * n_gy
    offsets = (1, -1, 2, -2)

    def to_row(step):
        return lax.rem(gy + step + n_gy, n_gy)

    def peer(step):
        return lax.rem(gx + step, n_gx)

    barrier = pltpu.get_barrier_semaphore()

    def greet(step, carry):
        pl.semaphore_signal(barrier, inc=1, device_id={"gx": peer(step)}, device_id_type=MESH)
        return carry

    for step in offsets:
        pl.semaphore_signal(barrier, inc=1, device_id={"gy": to_row(step)}, device_id_type=MESH)
    lax.fori_loop(1, n_gx, greet, 0)

    own_piece = pltpu.make_async_copy(
        prior_ref.at[:, :, pl.ds(pl.multiple_of(gx * lanes, lanes), lanes)],
        recv.at[pl.ds(gx * own_members, own_members)],
        own_sem.at[0],
    )
    own_obs = pltpu.make_async_copy(spread_ref, obs.at[pl.ds(0, members), pl.ds(2 * lanes, lanes)], own_sem.at[1])
    own_misfit = pltpu.make_async_copy(misfit_ref, obs_misfit.at[2], own_sem.at[2])
    own_line = pltpu.make_async_copy(line_ref, obs_line.at[2], own_sem.at[3])
    own_piece.start()
    own_obs.start()
    own_misfit.start()
    own_line.start()

    pl.semaphore_wait(barrier, n_gx - 1 + len(offsets))

    def obs_copies(k):
        step = offsets[k]
        slot = 2 - step
        ends = (
            (spread_ref, obs.at[pl.ds(0, members), pl.ds(slot * lanes, lanes)]),
            (misfit_ref, obs_misfit.at[slot]),
            (line_ref, obs_line.at[slot]),
        )
        return [
            pltpu.make_async_remote_copy(
                src_ref=src,
                dst_ref=dst,
                send_sem=obs_send.at[k, j],
                recv_sem=obs_recv.at[k, j],
                device_id={"gy": to_row(step)},
                device_id_type=MESH,
            )
            for j, (src, dst) in enumerate(ends)
        ]

    def piece(step):
        there = peer(step)
        return pltpu.make_async_remote_copy(
            src_ref=prior_ref.at[:, :, pl.ds(pl.multiple_of(there * lanes, lanes), lanes)],
            dst_ref=recv.at[pl.ds(gx * own_members, own_members)],
            send_sem=a2a_send.at[step],
            recv_sem=a2a_recv.at[step],
            device_id={"gx": there},
            device_id_type=MESH,
        )

    sends = [obs_copies(k) for k in range(len(offsets))]
    for k in (0, 1):
        for copy in sends[k]:
            copy.start()

    def send(step, carry):
        piece(step).start()
        return carry

    lax.fori_loop(1, n_gx, send, 0)
    for k in (2, 3):
        for copy in sends[k]:
            copy.start()

    own_obs.wait()
    own_misfit.wait()
    own_line.wait()

    def arrived(k):
        for copy in sends[k]:
            copy.wait_recv()

    arrived(0)
    arrived(1)

    def point_transform(i, carry):
        @pl.when(i == 2)
        def _():
            arrived(2)
            arrived(3)

        which = jnp.where(i == 2, -1, jnp.where(i == 3, 2, i))
        first = jnp.where(i == 2, 0, jnp.where(i == 3, 2, 1))
        point = 2 * gy + which
        centre = (point.astype(jnp.float32) + 0.5) * spacing
        local = []
        values = []
        for s in range(3):
            tile = gy + first + s - 2
            line = obs_line[first + s].astype(jnp.float32)
            position = (tile * rows).astype(jnp.float32) + line + 0.5
            distance = (position - centre) / float(rows)
            there = jnp.where(jnp.logical_and(tile >= 0, tile < n_gy), 1.0, 0.0)
            local.append(jnp.exp(-0.5 * distance * distance) * there)
            values.append(obs_misfit[first + s])
        locality = jnp.concatenate(local, axis=1)
        misfit = jnp.concatenate(values, axis=1)
        block = obs[:, pl.ds(pl.multiple_of(first * lanes, lanes), 3 * lanes)]
        scaled = (block.astype(jnp.float32) * locality).astype(jnp.bfloat16)
        gram = mm(block, scaled, NT)
        drive = mm(jnp.broadcast_to(misfit, (16, 3 * lanes)), scaled, NT)[:8]

        eye = jnp.where(
            lax.broadcasted_iota(jnp.int32, (members, members), 0)
            == lax.broadcasted_iota(jnp.int32, (members, members), 1),
            1.0,
            0.0,
        )
        m = eye + gram * (1.0 / (members - 1.0))
        sums = jnp.sum(jnp.abs(m), axis=0, keepdims=True)
        bound = jnp.max(sums, axis=1, keepdims=True)
        y = m * (1.0 / bound)
        yh, yl = halves(y)
        q = mm(yh, yh) + (mm(yh, yl) + mm(yl, yh))
        qh, ql = halves(q)
        r = 0.0625 * q - 0.5625 * y
        rh, rl = halves(r)
        z = 2.25 * eye - 2.4375 * y + 1.6875 * q + (mm(qh, rh) + (mm(qh, rl) + mm(ql, rh)))
        zh, zl = halves(z)

        def through(v):
            vh, vl = halves(v)
            both = jnp.concatenate([vh, vl], axis=0)
            p = mm(both, zh)
            return p[:8] + p[8:] + mm(both, zl)[:8]

        weights = through(through(drive))[:1] * (1.0 / (bound * (members - 1.0)))
        transforms[i] = z * lax.rsqrt(bound) + weights
        return carry

    lax.fori_loop(0, 4, point_transform, 0)

    pairs = ((0, -1), (0, 1), (0, 1), (1, 2))
    place = {0: 0, 1: 1, -1: 2, 2: 3}
    for row, (p, q) in enumerate(pairs):
        at = gy * rows + row
        wp = hat(at, 2 * gy + p, float(spacing), float(height))
        wq = hat(at, 2 * gy + q, float(spacing), float(height))
        mixed[row] = (wp * transforms[place[p]] + wq * transforms[place[q]]).astype(jnp.bfloat16)

    own_piece.wait()

    def land(step, carry):
        piece(step).wait_recv()
        return carry

    lax.fori_loop(1, n_gx, land, 0)

    wide[...] = recv.reshape(members * rows, lanes)[...].astype(jnp.float32)
    for row in range(rows):
        x = wide[pl.ds(row, members, stride=rows), :]
        mean = jnp.sum(x, axis=0, keepdims=True) * (1.0 / members)
        deviation = (x - mean).astype(jnp.bfloat16)
        wide[pl.ds(row, members, stride=rows), :] = mm(mixed[row], deviation) + mean
    out_ref[...] = wide[...].astype(jnp.bfloat16)

    def sent(step, carry):
        piece(step).wait_send()
        return carry

    lax.fori_loop(1, n_gx, sent, 0)
    for copies in sends:
        for copy in copies:
            copy.wait_send()


def solution(mesh):
    n_gx, n_gy = mesh.shape["gx"], mesh.shape["gy"]

    def on_device(prior, spread, misfit, line):
        members, _, lanes = spread.shape
        rows = prior.shape[1]
        out = pl.pallas_call(
            functools.partial(kernel, n_gx, n_gy),
            out_shape=jax.ShapeDtypeStruct((members * rows, lanes), jnp.bfloat16),
            in_specs=[pl.BlockSpec(memory_space=pl.ANY)] * 4,
            out_specs=pl.BlockSpec(memory_space=pltpu.VMEM),
            scratch_shapes=[
                pltpu.VMEM((members, rows, lanes), jnp.bfloat16),
                pltpu.VMEM((members, 5 * lanes), jnp.bfloat16),
                pltpu.VMEM((5, 1, lanes), jnp.bfloat16),
                pltpu.VMEM((5, 1, lanes), jnp.int32),
                pltpu.VMEM((4, members, members), jnp.float32),
                pltpu.VMEM((rows, members, members), jnp.bfloat16),
                pltpu.VMEM((members * rows, lanes), jnp.float32),
                pltpu.SemaphoreType.DMA((n_gx,)),
                pltpu.SemaphoreType.DMA((n_gx,)),
                pltpu.SemaphoreType.DMA((4, 3)),
                pltpu.SemaphoreType.DMA((4, 3)),
                pltpu.SemaphoreType.DMA((4,)),
            ],
            compiler_params=pltpu.CompilerParams(
                collective_id=0, has_side_effects=True, vmem_limit_bytes=48 * 1024 * 1024
            ),
            name="analysis",
        )(prior, spread.reshape(members, lanes), misfit, line)
        return out.reshape(members, rows, lanes)

    return jax.shard_map(
        on_device,
        mesh=mesh,
        in_specs=(P("gx", "gy", None), P(None, "gy", "gx"), P("gy", "gx"), P("gy", "gx")),
        out_specs=P(None, "gy", "gx"),
        check_vma=False,
    )
```

time: 94.9 us -> 45.4 us (0.48)
  the two profiles are of different devices: /device:TPU:6 before, /device:TPU:10 now
where the time goes in v1:
time: 45.4 us; the launch traced here: 45.2 us
  Pallas kernels  41.7 us (92%)
  local copies, waits for them, and re-layouts  3.41 us (8%)
    pallas_call x1, Pallas kernels, on_device(): pl.pallas_call(functools.partial(kernel, n_gx, n_gy), out_shape=jax.Shape...  41.7 us
    unnamed x9, local copies, waits for them, and re-layouts  3.41 us

profile of v1, /device:TPU:10, one launch (start us, length us, event | category | flops | bytes accessed | tf_op | source)
XLA Modules:
  0.0 45.2 jit_solution(11776681248162414953)
XLA Ops:
  0.0 0.0 copy-start.3
  0.0 0.0 copy-start.2
  0.0 0.7 %copy-done.3 = s32[1,128]{1,0:T(1,128)S(1)} copy-done((s32[1,128]{1,0:T(1,128)S(1)}, s32[1,128]{1,0:T(1,128)}, u32[]{:S(2)}) %copy-start.3) | copy-done | bytes 536
  0.7 0.0 copy-done.2
  0.7 0.0 copy-start
  0.7 1.0 %copy-done = bf16[16,4,4096]{2,1,0:T(4,128)(2,1)S(1)} copy-done((bf16[16,4,4096]{2,1,0:T(4,128)(2,1)S(1)}, bf16[16,4,4096]{2,1,0:T(4,128)(2,1)}, u32[]{:S(2)}) %copy-start) | copy-done | bytes 524312
  1.7 0.0 copy-start.1
  1.7 0.9 %copy-done.1 = bf16[512,1,128]{2,0,1:T(8,128)(2,1)S(1)} copy-done((bf16[512,1,128]{2,0,1:T(8,128)(2,1)S(1)}, bf16[512,1,128]{2,0,1:T(8,128)(2,1)}, u32[]{:S(2)}) %copy-start.1) | copy-done | bytes 131096
  2.6 41.7 %analysis.1 = bf16[2048,128]{1,0:T(8,128)(2,1)S(1)} custom-call(bf16[16,4,4096]{2,1,0:T(4,128)(2,1)S(1)} %copy-done, bf16[512,128]{1,0:T(8,128)(2,1)S(1)} %bitcast.3, bf16[1,128]{1,0:T(2,128)(2,1)S(1)} %copy-done.2, s32[1,128]{1,0:T(1,128)S(1)} %copy-done.3), custom_call_target="tpu_custom_call" | custom-call | tf_op jit(solution)/shard_map/analysis/pallas_call | solution.py:244
  44.4 0.8 %copy.6 = bf16[512,4,128]{2,1,0:T(4,128)(2,1)} copy(bf16[512,4,128]{2,1,0:T(4,128)(2,1)S(1)} %bitcast.2) | data formatting | bytes 1048576
Async XLA Ops:
  0.0 0.7 %copy-start.3 = (s32[1,128]{1,0:T(1,128)S(1)}, s32[1,128]{1,0:T(1,128)}, u32[]{:S(2)}) copy-start(s32[1,128]{1,0:T(1,128)} %line_ref.1) | copy-start | bytes 1540
  0.0 0.7 %copy-start.2 = (bf16[1,128]{1,0:T(2,128)(2,1)S(1)}, bf16[1,128]{1,0:T(2,128)(2,1)}, u32[]{:S(2)}) copy-start(bf16[1,128]{1,0:T(2,128)(2,1)} %misfit_ref.1) | copy-start | bytes 772
  0.7 1.0 %copy-start = (bf16[16,4,4096]{2,1,0:T(4,128)(2,1)S(1)}, bf16[16,4,4096]{2,1,0:T(4,128)(2,1)}, u32[]{:S(2)}) copy-start(bf16[16,4,4096]{2,1,0:T(4,128)(2,1)} %prior_ref.1) | copy-start | bytes 1572868
  1.7 0.9 %copy-start.1 = (bf16[512,1,128]{2,0,1:T(8,128)(2,1)S(1)}, bf16[512,1,128]{2,0,1:T(8,128)(2,1)}, u32[]{:S(2)}) copy-start(bf16[512,1,128]{2,0,1:T(8,128)(2,1)} %param.5) | copy-start | bytes 393220

commit v2 on v1

v2 whole, which is shorter than its diff:
```python
import functools

import jax
import jax.numpy as jnp
from jax import lax
from jax.experimental import pallas as pl
from jax.experimental.pallas import tpu as pltpu
from jax.sharding import PartitionSpec as P

MESH = pl.DeviceIdType.MESH
NT = (((1,), (1,)), ((), ()))
NN = (((1,), (0,)), ((), ()))
OFFSETS = (1, -1, 2, -2)


def mm(a, b, dims=NN):
    return lax.dot_general(a, b, dims, preferred_element_type=jnp.float32)


def halves(x):
    high = x.astype(jnp.bfloat16)
    return high, x - high.astype(jnp.float32)


def hat(row, point, spacing, height):
    r = jnp.clip(row.astype(jnp.float32) + 0.5, 0.5 * spacing, height - 0.5 * spacing)
    centre = (point.astype(jnp.float32) + 0.5) * spacing
    return jnp.maximum(0.0, 1.0 - jnp.abs(r - centre) / spacing)


def kernel(
    n_gx,
    n_gy,
    prior_ref,
    spread_ref,
    misfit_ref,
    line_ref,
    out_ref,
    recv,
    obs,
    obs_misfit,
    obs_line,
    eye,
    inner,
    mixed,
    wide,
    a2a_send,
    a2a_recv,
    obs_send,
    obs_recv,
    own_sem,
    go_sem,
    ack_sem,
):
    gx = lax.axis_index("gx")
    gy = lax.axis_index("gy")
    own_members, rows, _ = prior_ref.shape
    members, lanes = spread_ref.shape
    spacing = rows // 2
    height = rows * n_gy
    split = n_gy // 2
    leader = (n_gx // 8) * 5 - 1
    upper = gy >= split

    def to_row(step):
        return {"gy": gy + step}

    def peer(step):
        return lax.rem(gx + step, n_gx)

    exists = {step: jnp.logical_and(gy + step >= 0, gy + step < n_gy) for step in OFFSETS}
    crosses = {
        step: jnp.logical_and(exists[step], jnp.logical_xor(upper, gy + step >= split)) for step in OFFSETS
    }
    near = {step: jnp.logical_and(exists[step], jnp.logical_not(crosses[step])) for step in OFFSETS}

    def count(flags):
        return sum(flags[step].astype(jnp.int32) for step in OFFSETS)

    barrier = pltpu.get_barrier_semaphore()
    for step in OFFSETS:

        @pl.when(jnp.logical_and(exists[step], jnp.logical_or(upper, jnp.logical_not(crosses[step]))))
        def _():
            pl.semaphore_signal(barrier, inc=1, device_id=to_row(step), device_id_type=MESH)

    own_piece = pltpu.make_async_copy(
        prior_ref.at[:, :, pl.ds(pl.multiple_of(gx * lanes, lanes), lanes)],
        recv.at[pl.ds(gx * own_members, own_members)],
        own_sem.at[0],
    )
    own_obs = pltpu.make_async_copy(spread_ref, obs.at[:, pl.ds(2 * lanes, lanes)], own_sem.at[1])
    own_misfit = pltpu.make_async_copy(misfit_ref, obs_misfit.at[2], own_sem.at[2])
    own_line = pltpu.make_async_copy(line_ref, obs_line.at[2], own_sem.at[3])
    for copy in (own_piece, own_obs, own_misfit, own_line):
        copy.start()

    def obs_copies(k):
        step = OFFSETS[k]
        slot = 2 - step
        ends = (
            (spread_ref, obs.at[:, pl.ds(slot * lanes, lanes)]),
            (misfit_ref, obs_misfit.at[slot]),
            (line_ref, obs_line.at[slot]),
        )
        return [
            pltpu.make_async_remote_copy(
                src_ref=src,
                dst_ref=dst,
                send_sem=obs_send.at[k, j],
                recv_sem=obs_recv.at[k, j],
                device_id=to_row(step),
                device_id_type=MESH,
            )
            for j, (src, dst) in enumerate(ends)
        ]

    sends = [obs_copies(k) for k in range(len(OFFSETS))]

    def start_obs(k, flag):
        @pl.when(flag)
        def _():
            for copy in sends[k]:
                copy.start()

    def piece(step):
        there = peer(step)
        return pltpu.make_async_remote_copy(
            src_ref=prior_ref.at[:, :, pl.ds(pl.multiple_of(there * lanes, lanes), lanes)],
            dst_ref=recv.at[pl.ds(gx * own_members, own_members)],
            send_sem=a2a_send.at[step],
            recv_sem=a2a_recv.at[step],
            device_id={"gx": there},
            device_id_type=MESH,
        )

    expected = jnp.where(upper, count(near), count(exists))
    expected = expected + jnp.where(gx == leader, n_gx - 1, 0)
    pl.semaphore_wait(barrier, expected)

    for k, step in enumerate(OFFSETS):

        @pl.when(jnp.logical_and(crosses[step], jnp.logical_not(upper)))
        def _():
            pl.semaphore_signal(ack_sem, inc=1, device_id=to_row(step), device_id_type=MESH)

    for k, step in enumerate(OFFSETS):
        start_obs(k, jnp.logical_and(exists[step], jnp.logical_or(near[step], jnp.logical_not(upper))))

    @pl.when(gx != leader)
    def _():
        pl.semaphore_signal(barrier, inc=1, device_id={"gx": leader}, device_id_type=MESH)
        pl.semaphore_wait(go_sem, 1)

    @pl.when(gx == leader)
    def _():
        def go(step, carry):
            pl.semaphore_signal(go_sem, inc=1, device_id={"gx": peer(step)}, device_id_type=MESH)
            return carry

        lax.fori_loop(1, n_gx, go, 0)

    def send(t, carry):
        far = n_gx // 2 + ((t + 1) // 2) * (1 - 2 * lax.rem(t, 2))
        piece(far).start()
        return carry

    lax.fori_loop(0, n_gx - 1, send, 0)

    n_cross = count(crosses)

    @pl.when(jnp.logical_and(upper, n_cross > 0))
    def _():
        pl.semaphore_wait(ack_sem, n_cross)
        for k, step in enumerate(OFFSETS):
            start_obs(k, crosses[step])

    eye[...] = jnp.where(
        lax.broadcasted_iota(jnp.int32, (members, members), 0)
        == lax.broadcasted_iota(jnp.int32, (members, members), 1),
        1.0,
        0.0,
    )
    for step in OFFSETS:
        slot = 2 + step

        @pl.when(jnp.logical_not(exists[step]))
        def _():
            obs[:, slot * lanes : (slot + 1) * lanes] = jnp.zeros((members, lanes), jnp.bfloat16)
            obs_misfit[slot] = jnp.zeros((1, lanes), jnp.bfloat16)
            obs_line[slot] = jnp.zeros((1, lanes), jnp.int32)

    own_obs.wait()
    own_misfit.wait()
    own_line.wait()

    def arrived(k):
        @pl.when(exists[-OFFSETS[k]])
        def _():
            for copy in sends[k]:
                copy.wait_recv()

    def transform(which, first):
        point = 2 * gy + which
        centre = (point.astype(jnp.float32) + 0.5) * spacing
        local = []
        for s in range(first, first + 3):
            tile = gy + s - 2
            position = (tile * rows).astype(jnp.float32) + obs_line[s].astype(jnp.float32) + 0.5
            distance = (position - centre) / float(rows)
            there = jnp.where(jnp.logical_and(tile >= 0, tile < n_gy), 1.0, 0.0)
            local.append(jnp.exp(-0.5 * distance * distance) * there)
        locality = jnp.concatenate(local, axis=1)
        misfit = jnp.concatenate([obs_misfit[s] for s in range(first, first + 3)], axis=1)
        block = obs[:, first * lanes : (first + 3) * lanes]
        scaled = (block.astype(jnp.float32) * locality).astype(jnp.bfloat16)
        gram = mm(block, scaled, NT)
        drive = mm(jnp.broadcast_to(misfit, (16, 3 * lanes)), scaled, NT)[:8]

        m = eye[...] + gram * (1.0 / (members - 1.0))
        bound = jnp.max(jnp.sum(jnp.abs(m), axis=0, keepdims=True), axis=1, keepdims=True)
        y = m * (1.0 / bound)
        yh, yl = halves(y)
        q = mm(
            jnp.concatenate([yh, yh], axis=1),
            jnp.concatenate([yh, (yl + yl).astype(jnp.bfloat16)], axis=0),
        )
        r = 0.0625 * q - 0.5625 * y
        z = mm(q.astype(jnp.bfloat16), r.astype(jnp.bfloat16))
        z = 2.25 * eye[...] - 2.4375 * y + 1.6875 * q + z
        zh, zl = halves(z)
        zl = zl.astype(jnp.bfloat16)

        def through(v):
            vh, vl = halves(v)
            both = jnp.concatenate([vh, vl.astype(jnp.bfloat16)], axis=0)
            p = mm(both, zh)
            return p[:8] + p[8:] + mm(both, zl)[:8]

        weights = through(through(drive))[:1] * (1.0 / (bound * (members - 1.0)))
        return z * lax.rsqrt(bound) + weights

    def weight(row, which):
        return hat(gy * rows + row, 2 * gy + which, float(spacing), float(height))

    arrived(0)
    arrived(1)
    t0 = transform(0, 1)
    t1 = transform(1, 1)
    inner[0] = t0
    inner[1] = t1
    mixed[1] = (weight(1, 0) * t0 + weight(1, 1) * t1).astype(jnp.bfloat16)
    mixed[2] = (weight(2, 0) * t0 + weight(2, 1) * t1).astype(jnp.bfloat16)
    arrived(2)
    arrived(3)
    mixed[0] = (weight(0, 0) * inner[0] + weight(0, -1) * transform(-1, 0)).astype(jnp.bfloat16)
    mixed[3] = (weight(3, 1) * inner[1] + weight(3, 2) * transform(2, 2)).astype(jnp.bfloat16)

    own_piece.wait()

    def land(step, carry):
        piece(step).wait_recv()
        return carry

    lax.fori_loop(1, n_gx, land, 0)

    wide[...] = recv.reshape(members * rows, lanes)[...].astype(jnp.float32)
    for row in range(rows):
        x = wide[pl.ds(row, members, stride=rows), :]
        mean = jnp.sum(x, axis=0, keepdims=True) * (1.0 / members)
        deviation = (x - mean).astype(jnp.bfloat16)
        wide[pl.ds(row, members, stride=rows), :] = mm(mixed[row], deviation) + mean
    out_ref[...] = wide[...].astype(jnp.bfloat16)

    def sent(step, carry):
        piece(step).wait_send()
        return carry

    lax.fori_loop(1, n_gx, sent, 0)
    for k, step in enumerate(OFFSETS):

        @pl.when(exists[step])
        def _():
            for copy in sends[k]:
                copy.wait_send()


def solution(mesh):
    n_gx, n_gy = mesh.shape["gx"], mesh.shape["gy"]

    def on_device(prior, spread, misfit, line):
        members, _, lanes = spread.shape
        rows = prior.shape[1]
        out = pl.pallas_call(
            functools.partial(kernel, n_gx, n_gy),
            out_shape=jax.ShapeDtypeStruct((members * rows, lanes), jnp.bfloat16),
            in_specs=[pl.BlockSpec(memory_space=pltpu.HBM)] * 4,
            out_specs=pl.BlockSpec(memory_space=pltpu.VMEM),
            scratch_shapes=[
                pltpu.VMEM((members, rows, lanes), jnp.bfloat16),
                pltpu.VMEM((members, 5 * lanes), jnp.bfloat16),
                pltpu.VMEM((5, 1, lanes), jnp.bfloat16),
                pltpu.VMEM((5, 1, lanes), jnp.int32),
                pltpu.VMEM((members, members), jnp.float32),
                pltpu.VMEM((2, members, members), jnp.float32),
                pltpu.VMEM((rows, members, members), jnp.bfloat16),
                pltpu.VMEM((members * rows, lanes), jnp.float32),
                pltpu.SemaphoreType.DMA((n_gx,)),
                pltpu.SemaphoreType.DMA((n_gx,)),
                pltpu.SemaphoreType.DMA((4, 3)),
                pltpu.SemaphoreType.DMA((4, 3)),
                pltpu.SemaphoreType.DMA((4,)),
                pltpu.SemaphoreType.REGULAR,
                pltpu.SemaphoreType.REGULAR,
            ],
            compiler_params=pltpu.CompilerParams(
                collective_id=0, has_side_effects=True, vmem_limit_bytes=67043328
            ),
            name="analysis",
        )(prior, spread.reshape(members, lanes), misfit, line)
        return out.reshape(members, rows, lanes)

    return jax.shard_map(
        on_device,
        mesh=mesh,
        in_specs=(P("gx", "gy", None), P(None, "gy", "gx"), P("gy", "gx"), P("gy", "gx")),
        out_specs=P(None, "gy", "gx"),
        check_vma=False,
    )
```

time: 45.4 us -> 34.3 us (0.76)
  the two profiles are of different devices: /device:TPU:10 before, /device:TPU:135 now
where the time goes in v2:
time: 34.3 us; the launch traced here: 34.1 us
  Pallas kernels  32.1 us (94%)
  local copies, waits for them, and re-layouts  2.02 us (6%)
    pallas_call x1, Pallas kernels, on_device(): pl.pallas_call(functools.partial(kernel, n_gx, n_gy), out_shape=jax.Shape...  32.1 us
    unnamed x1, local copies, waits for them, and re-layouts  2.02 us

profile of v2, /device:TPU:135, one launch (start us, length us, event | category | flops | bytes accessed | tf_op | source)
XLA Modules:
  0.0 34.1 jit_solution(8614536086033917809)
XLA Ops:
  0.0 32.1 %analysis.1 = bf16[2048,128]{1,0:T(8,128)(2,1)} custom-call(bf16[16,4,4096]{2,1,0:T(4,128)(2,1)} %prior_ref.1, bf16[512,128]{1,0:T(8,128)(2,1)} %bitcast.3, bf16[1,128]{1,0:T(2,128)(2,1)} %misfit_ref.1, s32[1,128]{1,0:T(1,128)} %line_ref.1), custom_call_target="tpu_custom_call" | custom-call | tf_op jit(solution)/shard_map/analysis/pallas_call | solution.py:294
  32.1 2.0 %copy.6 = bf16[512,4,128]{2,1,0:T(4,128)(2,1)} copy(bf16[512,4,128]{2,1,0:T(4,128)(2,1)} %bitcast.2) | data formatting | bytes 1048576

commit v3 on v2

v3 whole, which is shorter than its diff:
```python
import functools

import jax
import jax.numpy as jnp
from jax import lax
from jax.experimental import pallas as pl
from jax.experimental.pallas import tpu as pltpu
from jax.sharding import PartitionSpec as P

MESH = pl.DeviceIdType.MESH
NT = (((1,), (1,)), ((), ()))
NN = (((1,), (0,)), ((), ()))
OFFSETS = (1, -1, 2, -2)


def mm(a, b, dims=NN):
    return lax.dot_general(a, b, dims, preferred_element_type=jnp.float32)


def halves(x):
    high = x.astype(jnp.bfloat16)
    return high, x - high.astype(jnp.float32)


def hat(row, point, spacing, height):
    r = jnp.clip(row.astype(jnp.float32) + 0.5, 0.5 * spacing, height - 0.5 * spacing)
    centre = (point.astype(jnp.float32) + 0.5) * spacing
    return jnp.maximum(0.0, 1.0 - jnp.abs(r - centre) / spacing)


def kernel(
    n_gx,
    n_gy,
    prior_ref,
    spread_ref,
    misfit_ref,
    line_ref,
    out_ref,
    recv,
    obs,
    obs_misfit,
    obs_line,
    inner,
    mixed,
    wide,
    a2a_send,
    a2a_recv,
    obs_send,
    obs_recv,
    own_sem,
    go_sem,
    ack_sem,
):
    gx = lax.axis_index("gx")
    gy = lax.axis_index("gy")
    own_members, rows, _ = prior_ref.shape
    members, lanes = spread_ref.shape
    spacing = rows // 2
    height = rows * n_gy
    split = n_gy // 2
    upper = gy >= split
    counts_gx = lax.rem(gx, 2) == 1
    counts_gy = lax.rem(gx, 2) == 0
    partner = gx + 1 - 2 * lax.rem(gx, 2)

    def to_row(step):
        return {"gy": gy + step}

    def peer(step):
        return lax.rem(gx + step, n_gx)

    exists = {step: jnp.logical_and(gy + step >= 0, gy + step < n_gy) for step in OFFSETS}
    crosses = [
        jnp.logical_and(exists[step], jnp.logical_and(upper, gy + step < split)) for step in OFFSETS
    ]
    across = functools.reduce(jnp.logical_or, crosses)
    neighbours = sum(exists[step].astype(jnp.int32) for step in OFFSETS)

    barrier = pltpu.get_barrier_semaphore()
    def greet(chip, carry):
        there = lax.rem(chip + gx // 2, n_gx // 2) * 2 + 1

        @pl.when(there != gx)
        def _():
            pl.semaphore_signal(barrier, inc=1, device_id={"gx": there}, device_id_type=MESH)

        return carry

    for step in OFFSETS:

        @pl.when(exists[step])
        def _():
            pl.semaphore_signal(
                barrier, inc=1, device_id={"gx": gx - lax.rem(gx, 2), "gy": gy + step}, device_id_type=MESH
            )

    @pl.when(counts_gx)
    def _():
        pl.semaphore_signal(barrier, inc=1, device_id={"gx": partner}, device_id_type=MESH)

    lax.fori_loop(0, n_gx // 2, greet, 0)

    own_piece = pltpu.make_async_copy(
        prior_ref.at[:, :, pl.ds(pl.multiple_of(gx * lanes, lanes), lanes)],
        recv.at[pl.ds(gx * own_members, own_members)],
        own_sem.at[0],
    )
    own_obs = pltpu.make_async_copy(
        spread_ref, obs.at[pl.ds(0, members), pl.ds(2 * lanes, lanes)], own_sem.at[1]
    )
    own_misfit = pltpu.make_async_copy(misfit_ref, obs_misfit.at[2], own_sem.at[2])
    own_line = pltpu.make_async_copy(line_ref, obs_line.at[2], own_sem.at[3])
    for copy in (own_piece, own_obs, own_misfit, own_line):
        copy.start()

    def obs_copies(k):
        step = OFFSETS[k]
        slot = 2 - step
        ends = (
            (spread_ref, obs.at[pl.ds(0, members), pl.ds(slot * lanes, lanes)]),
            (misfit_ref, obs_misfit.at[slot]),
            (line_ref, obs_line.at[slot]),
        )
        return [
            pltpu.make_async_remote_copy(
                src_ref=src,
                dst_ref=dst,
                send_sem=obs_send.at[k, j],
                recv_sem=obs_recv.at[k, j],
                device_id=to_row(step),
                device_id_type=MESH,
            )
            for j, (src, dst) in enumerate(ends)
        ]

    sends = [obs_copies(k) for k in range(len(OFFSETS))]

    def piece(step):
        there = peer(step)
        return pltpu.make_async_remote_copy(
            src_ref=prior_ref.at[:, :, pl.ds(pl.multiple_of(there * lanes, lanes), lanes)],
            dst_ref=recv.at[pl.ds(gx * own_members, own_members)],
            send_sem=a2a_send.at[step],
            recv_sem=a2a_recv.at[step],
            device_id={"gx": there},
            device_id_type=MESH,
        )

    def send(t, carry):
        far = n_gx // 2 + ((n_gx - 1 - t) // 2) * (1 - 2 * lax.rem(n_gx - 2 - t, 2))
        piece(far).start()
        return carry

    def start_obs():
        for k, step in enumerate(OFFSETS):

            @pl.when(exists[step])
            def _():
                for copy in sends[k]:
                    copy.start()

    def exchange_gx():
        @pl.when(counts_gx)
        def _():
            pl.semaphore_wait(barrier, n_gx - 1)
            pl.semaphore_signal(go_sem, inc=1, device_id={"gx": partner}, device_id_type=MESH)

        @pl.when(counts_gy)
        def _():
            pl.semaphore_wait(go_sem, 1)

        lax.fori_loop(0, n_gx - 1, send, 0)

    def exchange_gy():
        @pl.when(counts_gy)
        def _():
            pl.semaphore_wait(barrier, 1 + 2 * neighbours)
            pl.semaphore_signal(ack_sem, inc=1, device_id={"gx": partner}, device_id_type=MESH)

        @pl.when(counts_gx)
        def _():
            pl.semaphore_wait(ack_sem, 1)

        start_obs()

    middle = jnp.logical_and(gx // (n_gx // 8) // 2 == 2, jnp.logical_or(gy < split - 2, gy >= split))
    gx_first = jnp.logical_or(across, middle)

    @pl.when(gx_first)
    def _():
        exchange_gx()
        exchange_gy()

    @pl.when(jnp.logical_not(gx_first))
    def _():
        exchange_gy()
        exchange_gx()

    for step in OFFSETS:
        slot = 2 + step

        @pl.when(jnp.logical_not(exists[step]))
        def _():
            obs[:members, slot * lanes : (slot + 1) * lanes] = jnp.zeros((members, lanes), jnp.bfloat16)
            obs_misfit[slot] = jnp.zeros((1, lanes), jnp.bfloat16)
            obs_line[slot] = jnp.zeros((1, lanes), jnp.int32)

    own_obs.wait()
    own_misfit.wait()
    own_line.wait()

    def arrived(k):
        @pl.when(exists[-OFFSETS[k]])
        def _():
            for copy in sends[k]:
                copy.wait_recv()

    def transform(which, first):
        point = 2 * gy + which
        centre = (point.astype(jnp.float32) + 0.5) * spacing
        local = []
        for s in range(first, first + 3):
            tile = gy + s - 2
            position = (tile * rows).astype(jnp.float32) + obs_line[s].astype(jnp.float32) + 0.5
            distance = (position - centre) / float(rows)
            there = jnp.where(jnp.logical_and(tile >= 0, tile < n_gy), 1.0, 0.0)
            local.append(jnp.exp(-0.5 * distance * distance) * there)
        locality = jnp.concatenate(local, axis=1)
        for s in range(first, first + 3):
            obs[members:, s * lanes : (s + 1) * lanes] = jnp.broadcast_to(obs_misfit[s], (16, lanes))
        block = obs[:, first * lanes : (first + 3) * lanes]
        scaled = (block[:members].astype(jnp.float32) * locality).astype(jnp.bfloat16)
        both = mm(block, scaled, NT)
        gram, drive = both[:members], both[members : members + 8]

        n = members - 1.0
        bound = 1.0 + jnp.max(jnp.sum(jnp.abs(gram), axis=0, keepdims=True), axis=1, keepdims=True) / n
        a = 1.0 / bound
        b = a / n
        z0 = 2.25 + a * (-2.4375 + a * (1.6875 + a * (-0.5625 + a * 0.0625)))
        z1 = -2.4375 + a * (3.375 + a * (-1.6875 + a * 0.25))
        z2 = 1.6875 + a * (-1.6875 + a * 0.375)
        z3 = -0.5625 + a * 0.25
        root = lax.rsqrt(bound)
        high = gram.astype(jnp.bfloat16)
        square = mm(high, high)
        inside = square + (z3 * 16.0 / b) * gram
        fourth = mm(square.astype(jnp.bfloat16), inside.astype(jnp.bfloat16))
        b2 = b * b
        t = (root * z1 * b) * gram + (root * z2 * b2) * square + (root * 0.0625 * b2 * b2) * fourth
        th = t.astype(jnp.bfloat16)

        def through(v):
            vh, vl = halves(v)
            both = jnp.concatenate([vh, vl.astype(jnp.bfloat16)], axis=0)
            p = mm(both, th)
            return (p[:8] + p[8:]) * (bound * root) + z0 * v

        weights = through(drive)
        weights = through(weights) / (bound * n)
        return t, weights[:1], z0 * root

    def weight(row, which):
        return hat(gy * rows + row, 2 * gy + which, float(spacing), float(height))

    def mix(row, first, second):
        (p, t, v, d), (p2, t2, v2, d2) = first, second
        wp, wq = weight(row, p), weight(row, p2)
        mixed[row] = (wp * t + wq * t2 + (wp * v + wq * v2)).astype(jnp.bfloat16)
        return wp * d + wq * d2

    arrived(0)
    arrived(1)
    (t0, v0, d0), (t1, v1, d1) = transform(0, 1), transform(1, 1)
    inner[0] = t0
    inner[1] = t1
    k1 = mix(1, (0, t0, v0, d0), (1, t1, v1, d1))
    k2 = mix(2, (0, t0, v0, d0), (1, t1, v1, d1))
    arrived(2)
    arrived(3)
    before, after = transform(-1, 0), transform(2, 2)
    k0 = mix(0, (0, inner[0], v0, d0), (-1, *before))
    k3 = mix(3, (1, inner[1], v1, d1), (2, *after))

    own_piece.wait()

    def land(step, carry):
        piece(step).wait_recv()
        return carry

    lax.fori_loop(1, n_gx, land, 0)

    wide[...] = recv.reshape(members * rows, lanes)[...].astype(jnp.float32)
    for row, diagonal in enumerate((k0, k1, k2, k3)):
        x = wide[pl.ds(row, members, stride=rows), :]
        mean = jnp.sum(x, axis=0, keepdims=True) * (1.0 / members)
        y = mm(mixed[row], (x - mean).astype(jnp.bfloat16))
        x = wide[pl.ds(row, members, stride=rows), :]
        wide[pl.ds(row, members, stride=rows), :] = y + (diagonal * x + (mean - diagonal * mean))
    out_ref[...] = wide[...].astype(jnp.bfloat16)

    def sent(step, carry):
        piece(step).wait_send()
        return carry

    lax.fori_loop(1, n_gx, sent, 0)
    for k, step in enumerate(OFFSETS):

        @pl.when(exists[step])
        def _():
            for copy in sends[k]:
                copy.wait_send()


def solution(mesh):
    n_gx, n_gy = mesh.shape["gx"], mesh.shape["gy"]

    def on_device(prior, spread, misfit, line):
        members, _, lanes = spread.shape
        rows = prior.shape[1]
        out = pl.pallas_call(
            functools.partial(kernel, n_gx, n_gy),
            out_shape=jax.ShapeDtypeStruct((members * rows, lanes), jnp.bfloat16),
            in_specs=[pl.BlockSpec(memory_space=pltpu.HBM)] * 4,
            out_specs=pl.BlockSpec(memory_space=pltpu.VMEM),
            scratch_shapes=[
                pltpu.VMEM((members, rows, lanes), jnp.bfloat16),
                pltpu.VMEM((members + 16, 5 * lanes), jnp.bfloat16),
                pltpu.VMEM((5, 1, lanes), jnp.bfloat16),
                pltpu.VMEM((5, 1, lanes), jnp.int32),
                pltpu.VMEM((2, members, members), jnp.float32),
                pltpu.VMEM((rows, members, members), jnp.bfloat16),
                pltpu.VMEM((members * rows, lanes), jnp.float32),
                pltpu.SemaphoreType.DMA((n_gx,)),
                pltpu.SemaphoreType.DMA((n_gx,)),
                pltpu.SemaphoreType.DMA((4, 3)),
                pltpu.SemaphoreType.DMA((4, 3)),
                pltpu.SemaphoreType.DMA((4,)),
                pltpu.SemaphoreType.REGULAR,
                pltpu.SemaphoreType.REGULAR,
            ],
            compiler_params=pltpu.CompilerParams(
                collective_id=0, has_side_effects=True, vmem_limit_bytes=67043328
            ),
            name="analysis",
        )(prior, spread.reshape(members, lanes), misfit, line)
        return out.reshape(members, rows, lanes)

    return jax.shard_map(
        on_device,
        mesh=mesh,
        in_specs=(P("gx", "gy", None), P(None, "gy", "gx"), P("gy", "gx"), P("gy", "gx")),
        out_specs=P(None, "gy", "gx"),
        check_vma=False,
    )
```

time: 34.3 us -> 31.1 us (0.907)
  the two profiles are of different devices: /device:TPU:135 before, /device:TPU:1 now
where the time goes in v3:
time: 31.1 us; the launch traced here: 30.9 us
  Pallas kernels  28.9 us (93%)
  local copies, waits for them, and re-layouts  2.02 us (6%)
    pallas_call x1, Pallas kernels, on_device(): pl.pallas_call(functools.partial(kernel, n_gx, n_gy), out_shape=jax.Shape...  28.9 us
    unnamed x1, local copies, waits for them, and re-layouts  2.02 us

profile of v3, /device:TPU:1, one launch (start us, length us, event | category | flops | bytes accessed | tf_op | source)
XLA Modules:
  0.0 30.9 jit_solution(2124967160585155930)
XLA Ops:
  0.0 28.9 %analysis.1 = bf16[2048,128]{1,0:T(8,128)(2,1)} custom-call(bf16[16,4,4096]{2,1,0:T(4,128)(2,1)} %prior_ref.1, bf16[512,128]{1,0:T(8,128)(2,1)} %bitcast.3, bf16[1,128]{1,0:T(2,128)(2,1)} %misfit_ref.1, s32[1,128]{1,0:T(1,128)} %line_ref.1), custom_call_target="tpu_custom_call" | custom-call | tf_op jit(solution)/shard_map/analysis/pallas_call | solution.py:321
  28.9 2.0 %copy.6 = bf16[512,4,128]{2,1,0:T(4,128)(2,1)} copy(bf16[512,4,128]{2,1,0:T(4,128)(2,1)} %bitcast.2) | data formatting | bytes 1048576

commit v4 on v3

--- a/solution.py
+++ b/solution.py
@@ -50,6 +50,7 @@
     own_sem,
     go_sem,
     ack_sem,
+    near_sem,
 ):
     gx = lax.axis_index("gx")
     gy = lax.axis_index("gy")
@@ -59,6 +60,7 @@
     height = rows * n_gy
     split = n_gy // 2
     upper = gy >= split
+
     counts_gx = lax.rem(gx, 2) == 1
     counts_gy = lax.rem(gx, 2) == 0
     partner = gx + 1 - 2 * lax.rem(gx, 2)
@@ -70,11 +72,17 @@
         return lax.rem(gx + step, n_gx)
 
     exists = {step: jnp.logical_and(gy + step >= 0, gy + step < n_gy) for step in OFFSETS}
-    crosses = [
-        jnp.logical_and(exists[step], jnp.logical_and(upper, gy + step < split)) for step in OFFSETS
-    ]
-    across = functools.reduce(jnp.logical_or, crosses)
-    neighbours = sum(exists[step].astype(jnp.int32) for step in OFFSETS)
+    crosses = {step: jnp.logical_xor(upper, gy + step >= split) for step in OFFSETS}
+    early = {
+        step: jnp.logical_and(exists[step], crosses[step] if step > 0 else jnp.logical_not(crosses[step]))
+        for step in OFFSETS
+    }
+    late = {step: jnp.logical_and(exists[step], jnp.logical_not(early[step])) for step in OFFSETS}
+    late_near = {step: jnp.logical_and(late[step], jnp.logical_not(crosses[step])) for step in OFFSETS}
+    late_across = {step: jnp.logical_and(late[step], crosses[step]) for step in OFFSETS}
+
+    def count(flags):
+        return sum(flags[step].astype(jnp.int32) for step in OFFSETS)
 
     barrier = pltpu.get_barrier_semaphore()
     def greet(chip, carry):
@@ -88,7 +96,7 @@
 
     for step in OFFSETS:
 
-        @pl.when(exists[step])
+        @pl.when(late[step])
         def _():
             pl.semaphore_signal(
                 barrier, inc=1, device_id={"gx": gx - lax.rem(gx, 2), "gy": gy + step}, device_id_type=MESH
@@ -147,14 +155,22 @@
         )
 
     def send(t, carry):
-        far = n_gx // 2 + ((n_gx - 1 - t) // 2) * (1 - 2 * lax.rem(n_gx - 2 - t, 2))
-        piece(far).start()
+        place = t // 4
+        row = lax.rem(((place + 1) // 2) * (2 * lax.rem(place, 2) - 1) + n_gx, n_gx // 4)
+        row = jnp.where(place == 5, 4, jnp.where(place == 6, 3, jnp.where(place == 7, 5, row)))
+        there = row * 4 + lax.rem(t + gx, 4)
+        step = lax.rem(there - gx + n_gx, n_gx)
+
+        @pl.when(step != 0)
+        def _():
+            piece(step).start()
+
         return carry
 
-    def start_obs():
+    def start_obs(flags):
         for k, step in enumerate(OFFSETS):
 
-            @pl.when(exists[step])
+            @pl.when(flags[step])
             def _():
                 for copy in sends[k]:
                     copy.start()
@@ -169,32 +185,54 @@
         def _():
             pl.semaphore_wait(go_sem, 1)
 
-        lax.fori_loop(0, n_gx - 1, send, 0)
-
-    def exchange_gy():
-        @pl.when(counts_gy)
-        def _():
-            pl.semaphore_wait(barrier, 1 + 2 * neighbours)
-            pl.semaphore_signal(ack_sem, inc=1, device_id={"gx": partner}, device_id_type=MESH)
-
-        @pl.when(counts_gx)
-        def _():
-            pl.semaphore_wait(ack_sem, 1)
-
-        start_obs()
-
-    middle = jnp.logical_and(gx // (n_gx // 8) // 2 == 2, jnp.logical_or(gy < split - 2, gy >= split))
-    gx_first = jnp.logical_or(across, middle)
-
-    @pl.when(gx_first)
+        lax.fori_loop(0, n_gx, send, 0)
+
+    def say_here(step, core):
+        pl.semaphore_signal(
+            near_sem.at[crosses[step].astype(jnp.int32)],
+            inc=1,
+            device_id={"gx": gx - lax.rem(gx, 2) + core, "gy": gy + step},
+            device_id_type=MESH,
+        )
+
+    @pl.when(counts_gy)
+    def _():
+        pl.semaphore_wait(barrier, 1 + 2 * count(early))
+        pl.semaphore_signal(ack_sem, inc=1, device_id={"gx": partner}, device_id_type=MESH)
+        for step in OFFSETS:
+
+            @pl.when(early[step])
+            def _():
+                say_here(step, 0)
+                say_here(step, 1)
+
+    @pl.when(counts_gx)
+    def _():
+        pl.semaphore_wait(ack_sem, 1)
+
+    second = {step: jnp.logical_and(early[step], gy == split - 2) if step == 2 else False for step in OFFSETS}
+    start_obs({step: jnp.logical_and(early[step], jnp.logical_not(second[step])) for step in OFFSETS})
+
+    middle = jnp.logical_and(gx // (n_gx // 8) // 2 == 2, jnp.logical_or(gy < split - 2, upper))
+
+    @pl.when(middle)
     def _():
         exchange_gx()
-        exchange_gy()
-
-    @pl.when(jnp.logical_not(gx_first))
-    def _():
-        exchange_gy()
+
+    @pl.when(count(late_near) > 0)
+    def _():
+        pl.semaphore_wait(near_sem.at[0], count(late_near))
+
+    start_obs({step: jnp.logical_or(late_near[step], second[step]) for step in OFFSETS})
+
+    @pl.when(jnp.logical_not(middle))
+    def _():
         exchange_gx()
+
+    @pl.when(count(late_across) > 0)
+    def _():
+        pl.semaphore_wait(near_sem.at[1], count(late_across))
+        start_obs(late_across)
 
     for step in OFFSETS:
         slot = 2 + step
@@ -282,6 +320,18 @@
     k0 = mix(0, (0, inner[0], v0, d0), (-1, *before))
     k3 = mix(3, (1, inner[1], v1, d1), (2, *after))
 
+    def sent(step, carry):
+        piece(step).wait_send()
+        return carry
+
+    lax.fori_loop(1, n_gx, sent, 0)
+    for k, step in enumerate(OFFSETS):
+
+        @pl.when(exists[step])
+        def _():
+            for copy in sends[k]:
+                copy.wait_send()
+
     own_piece.wait()
 
     def land(step, carry):
@@ -298,18 +348,6 @@
         x = wide[pl.ds(row, members, stride=rows), :]
         wide[pl.ds(row, members, stride=rows), :] = y + (diagonal * x + (mean - diagonal * mean))
     out_ref[...] = wide[...].astype(jnp.bfloat16)
-
-    def sent(step, carry):
-        piece(step).wait_send()
-        return carry
-
-    lax.fori_loop(1, n_gx, sent, 0)
-    for k, step in enumerate(OFFSETS):
-
-        @pl.when(exists[step])
-        def _():
-            for copy in sends[k]:
-                copy.wait_send()
 
 
 def solution(mesh):
@@ -338,6 +376,7 @@
                 pltpu.SemaphoreType.DMA((4,)),
                 pltpu.SemaphoreType.REGULAR,
                 pltpu.SemaphoreType.REGULAR,
+                pltpu.SemaphoreType.REGULAR((2,)),
             ],
             compiler_params=pltpu.CompilerParams(
                 collective_id=0, has_side_effects=True, vmem_limit_bytes=67043328

time: 31.1 us -> 30.5 us (0.981)
  the two profiles are of different devices: /device:TPU:1 before, /device:TPU:46 now
where the time goes in v4:
time: 30.5 us; the launch traced here: 30.3 us
  Pallas kernels  28.3 us (93%)
  local copies, waits for them, and re-layouts  2.02 us (7%)
    pallas_call x1, Pallas kernels, on_device(): pl.pallas_call(functools.partial(kernel, n_gx, n_gy), out_shape=jax.Shape...  28.3 us
    unnamed x1, local copies, waits for them, and re-layouts  2.02 us

profile of v4, /device:TPU:46, one launch (start us, length us, event | category | flops | bytes accessed | tf_op | source)
XLA Modules:
  0.0 30.3 jit_solution(9125659849795439558)
XLA Ops:
  0.0 28.3 %analysis.1 = bf16[2048,128]{1,0:T(8,128)(2,1)} custom-call(bf16[16,4,4096]{2,1,0:T(4,128)(2,1)} %prior_ref.1, bf16[512,128]{1,0:T(8,128)(2,1)} %bitcast.3, bf16[1,128]{1,0:T(2,128)(2,1)} %misfit_ref.1, s32[1,128]{1,0:T(1,128)} %line_ref.1), custom_call_target="tpu_custom_call" | custom-call | tf_op jit(solution)/shard_map/analysis/pallas_call | solution.py:359
  28.3 2.0 %copy.6 = bf16[512,4,128]{2,1,0:T(4,128)(2,1)} copy(bf16[512,4,128]{2,1,0:T(4,128)(2,1)} %bitcast.2) | data formatting | bytes 1048576
